TPU v7x, 32 devices: a whole 2x2x4 slice. The times are simulated.
32 devices in a mesh: floor: 4 (over y, x), zone: 8 (over z, core).
Axes of the slice: x: 2, y: 2, z: 4, core: 2. Of those that a mesh axis runs over, the one named last changes fastest.
Arguments:
- factor: float32 [512, 96, 384], P(('floor', 'zone')), may hold values from -0.625 to 0.625
- plant_map: float32 [512, 96, 384], P(('floor', 'zone')), may hold values from -0.4082483 to 0.4082483
- offset: float32 [512, 384], P(('floor', 'zone')), may hold values from -10 to 10
- start_plan: float32 [512, 384], P(('floor', 'zone')), may hold values from -10 to 10
- demand: float32 [4, 48], replicated, may hold values from -768 to 768
- start_price: float32 [4, 48], replicated, may hold values from -6 to 6
- start_multiplier: float32 [512, 48], P(('floor', 'zone')), may hold values from -6 to 6
- neighbors: int32 [512, 4], P(('floor', 'zone')), may hold values from 0 to 127
- loop_of_zone: int32 [512], P(('floor', 'zone')), may hold values from 0 to 3
Outputs:
- control: float32 [512, 384], P(('floor', 'zone'))
- price: float32 [4, 48], replicated
- multiplier: float32 [512, 48], P(('floor', 'zone'))
Inputs may be any that keep to these rules, and one draw needn't show every extreme that they name: `neighbors`: indices count zones within the zone's own floor of 128 consecutive zones.
All inputs are finite; a program needn't handle non-finite values.
Results may differ from a plain program's by a relative error of at most 0.0001.
Values sent between devices are 32-bit elements; how exact they have to be, the bound alone decides.
No kernel may reach another device: no remote copies, remote signals or barrier semaphores. Data moves between devices by JAX's collectives and lax.ppermute only.
A program may use at most 64 MiB of HBM per device.

v0:
```python
import jax
import jax.numpy as jnp
from jax import lax
from jax.sharding import PartitionSpec as P

HORIZON = 48
NEIGHBORS = 4
LOOPS = 4
ITERS = 2


def select_rows(neighbors, count):
    columns = jnp.arange(count, dtype=jnp.int32)
    picks = (neighbors[:, :, None] == columns[None, None, :]).astype(jnp.float32)
    return jnp.sum(picks, axis=1) / NEIGHBORS


def local(
    factor,
    plant_map,
    offset,
    start_plan,
    demand,
    start_price,
    start_multiplier,
    neighbors,
    loop_of_zone,
):
    control = start_plan
    price = start_price
    multiplier = start_multiplier
    zones_here = control.shape[0]
    zones_all = zones_here * lax.axis_size("floor") * lax.axis_size("zone")
    onehot = (loop_of_zone[:, None] == jnp.arange(LOOPS, dtype=jnp.int32)[None, :]).astype(
        jnp.float32
    )
    for step in range(ITERS):
        outputs = jnp.einsum("zkv,zv->zk", plant_map, control, precision=lax.Precision.HIGHEST)
        shares = outputs[:, :HORIZON]
        bound = outputs[:, HORIZON:]
        partial_load = jnp.dot(onehot.T, shares, precision=lax.Precision.HIGHEST)
        floor_load = lax.psum(partial_load, "zone")
        total = lax.psum(floor_load, "floor")
        excess = (total - demand) * (LOOPS / zones_all)
        shift = jnp.dot(onehot, excess + price, precision=lax.Precision.HIGHEST)
        price = price + excess
        target_share = shares - shift
        floor_bound = lax.all_gather(bound, "zone", axis=0, tiled=True)
        weights = select_rows(neighbors, floor_bound.shape[0])
        near = jnp.dot(weights, floor_bound, precision=lax.Precision.HIGHEST)
        target_bound = (bound + near) / 2.0 - multiplier
        multiplier = multiplier + (bound - near) / 2.0
        target = jnp.concatenate([target_share, target_bound], axis=1)
        control = (
            0.8 * jnp.einsum("zkv,zk->zv", factor, target, precision=lax.Precision.HIGHEST) - offset
        )
    return (control, price, multiplier)


def solution(mesh):
    placed = (
        P(("floor", "zone"), None, None),
        P(("floor", "zone"), None, None),
        P(("floor", "zone"), None),
        P(("floor", "zone"), None),
        P(),
        P(),
        P(("floor", "zone"), None),
        P(("floor", "zone"), None),
        P(("floor", "zone")),
    )
    return jax.shard_map(
        local,
        mesh=mesh,
        in_specs=placed,
        out_specs=(P(("floor", "zone"), None), P(), P(("floor", "zone"), None)),
        check_vma=False,
    )
```

profile of v0, /device:TPU:0, one launch (start us, length us, event | category | flops | bytes accessed | tf_op | source)
XLA Modules:
  0.0 91.8 jit_solution(17976281189199001725)
XLA Ops:
  0.6 0.0 copy-start
  0.6 0.0 copy-start.3
  0.7 0.0 copy-start.4
  0.7 0.0 copy-start.8
  0.7 0.0 copy-start.5
  0.7 0.0 copy-start.6
  0.7 0.0 copy-start.2
  0.7 4.4 %fusion.5 = f32[16,1,96]{2,1,0:T(1,128)S(1)} fusion(f32[16,96,384]{2,1,0:T(8,128)} %param.10, f32[16,384,1]{1,0,2:T(8,128)} %bitcast.43), kind=kOutput, calls=%fused_computation.11 | convolution fusion | flops 7077888 | bytes 2390016 | tf_op jit(solution)/shard_map/zkv,zv->zk/dot_general | solution.py:38
  5.1 0.1 slice.17
  5.2 15.7 %all_gather.6 = f32[128,48]{1,0:T(8,128)S(1)} all-gather(f32[16,48]{1,0:T(8,128)S(1)} %slice.17), channel_id=1, replica_groups=mesh['floor'=4,'zone'=8] {'zone'}, dimensions={0}, use_global_device_ids=true | all-gather | bytes 27648 | tf_op jit(solution)/shard_map/all_gather | solution.py:48
  20.9 0.0 copy-done.4
  20.9 0.1 convert_reduce_fusion
  21.0 0.0 copy-done.3
  21.0 0.2 multiply_subtract_fusion.1
  21.1 0.0 copy-done.8
  21.1 0.3 fusion.8
  21.4 16.9 %psum.28 = f32[4,48]{1,0:T(4,128)S(1)} all-reduce(f32[4,48]{1,0:T(4,128)S(1)} %fusion.8), channel_id=1, replica_groups=mesh['floor'=4,'zone'=8] {'zone'}, use_global_device_ids=true, to_apply=%region_0.0 | all-reduce | flops 192 | bytes 1536 | tf_op jit(solution)/shard_map/psum | solution.py:42
  38.3 9.9 %psum.29 = f32[4,48]{1,0:T(4,128)S(1)} all-reduce(f32[4,48]{1,0:T(4,128)S(1)} %psum.28), channel_id=1, replica_groups=mesh['floor'=4,'zone'=8] {'floor'}, use_global_device_ids=true, to_apply=%region_1.0 | all-reduce | flops 192 | bytes 1536 | tf_op jit(solution)/shard_map/psum | solution.py:43
  48.2 0.0 copy-done.5
  48.2 0.0 copy-done.6
  48.2 0.0 copy-start.1
  48.2 0.2 convolution_subtract_fusion.1
  48.4 0.1 pad_maximum_fusion
  48.5 0.0 copy-done
  48.5 1.4 %fusion.24 = f32[16,1,384]{2,1,0:T(1,128)S(1)} fusion(f32[16,96,1]{1,2,0:T(1,128)S(1)} %bitcast.41, f32[16,96,384]{2,1,0:T(8,128)S(1)} %copy-done), kind=kOutput, calls=%fused_computation.39 | convolution fusion | flops 7077888 | bytes 2390016 | tf_op jit(solution)/shard_map/zkv,zk->zv/dot_general | solution.py:55
  49.9 0.0 copy-done.2
  49.9 0.0 copy-done.1
  49.9 2.6 %fusion.3 = f32[16,1,96]{2,1,0:T(1,128)S(1)} fusion(f32[16,96,384]{2,1,0:T(8,128)S(1)} %copy-done.1, f32[16,384,1]{1,0,2:T(8,128)S(1)} %fusion.2), kind=kOutput, calls=%fused_computation.9 | convolution fusion | flops 7077888 | bytes 2390016 | tf_op jit(solution)/shard_map/zkv,zv->zk/dot_general | solution.py:38
  52.5 0.1 slice.19
  52.6 14.0 %all_gather.7 = f32[128,48]{1,0:T(8,128)S(1)} all-gather(f32[16,48]{1,0:T(8,128)S(1)} %slice.19), channel_id=1, replica_groups=mesh['floor'=4,'zone'=8] {'zone'}, dimensions={0}, use_global_device_ids=true | all-gather | bytes 27648 | tf_op jit(solution)/shard_map/all_gather | solution.py:48
  66.6 0.8 multiply_add_fusion
  67.4 0.3 fusion.7
  67.6 13.9 %psum.30 = f32[4,48]{1,0:T(4,128)S(1)} all-reduce(f32[4,48]{1,0:T(4,128)S(1)} %fusion.7), channel_id=1, replica_groups=mesh['floor'=4,'zone'=8] {'zone'}, use_global_device_ids=true, to_apply=%region_3.0 | all-reduce | flops 192 | bytes 1536 | tf_op jit(solution)/shard_map/psum | solution.py:42
  81.5 7.9 %psum.31 = f32[4,48]{1,0:T(4,128)S(1)} all-reduce(f32[4,48]{1,0:T(4,128)S(1)} %psum.30), channel_id=1, replica_groups=mesh['floor'=4,'zone'=8] {'floor'}, use_global_device_ids=true, to_apply=%region_4.0 | all-reduce | flops 192 | bytes 1536 | tf_op jit(solution)/shard_map/psum | solution.py:43
  89.5 0.0 copy-start.7
  89.5 0.2 convolution_subtract_fusion
  89.7 0.1 pad_maximum_fusion.1
  89.8 1.4 %fusion.25 = f32[16,1,384]{2,1,0:T(1,128)S(1)} fusion(f32[16,96,1]{1,2,0:T(1,128)S(1)} %bitcast.42, f32[16,96,384]{2,1,0:T(8,128)S(1)} %copy-done), kind=kOutput, calls=%fused_computation.40 | convolution fusion | flops 7077888 | bytes 2390016 | tf_op jit(solution)/shard_map/zkv,zk->zv/dot_general | solution.py:55
  91.2 0.6 fusion
  91.8 0.0 copy-done.7
  (2 shorter events, 0.0 us)
Async XLA Ops:
  0.6 47.8 %copy-start = (f32[16,96,384]{2,1,0:T(8,128)S(1)}, f32[16,96,384]{2,1,0:T(8,128)}, u32[]{:S(2)}) copy-start(f32[16,96,384]{2,1,0:T(8,128)} %param.9) | copy-start | bytes 7077892
  0.6 20.3 %copy-start.3 = (f32[16,48]{1,0:T(8,128)S(1)}, f32[16,48]{1,0:T(8,128)}, u32[]{:S(2)}) copy-start(f32[16,48]{1,0:T(8,128)} %param.15) | copy-start | bytes 9220
  0.7 20.2 %copy-start.4 = (s32[16,4]{0,1:T(4,128)S(1)}, s32[16,4]{0,1:T(4,128)}, u32[]{:S(2)}) copy-start(s32[16,4]{0,1:T(4,128)} %param.16) | copy-start | bytes 772
  0.7 20.5 %copy-start.8 = (s32[16]{0:T(128)S(1)}, s32[16]{0:T(128)}, u32[]{:S(2)}) copy-start(s32[16]{0:T(128)} %param.17) | copy-start | bytes 196
  0.7 47.5 %copy-start.5 = (f32[4,48]{1,0:T(4,128)S(1)}, f32[4,48]{1,0:T(4,128)}, u32[]{:S(2)}) copy-start(f32[4,48]{1,0:T(4,128)} %param.14) | copy-start | bytes 2308
  0.7 47.5 %copy-start.6 = (f32[4,48]{1,0:T(4,128)S(1)}, f32[4,48]{1,0:T(4,128)}, u32[]{:S(2)}) copy-start(f32[4,48]{1,0:T(4,128)} %param.13) | copy-start | bytes 2308
  0.7 49.2 %copy-start.2 = (f32[16,384]{1,0:T(8,128)S(1)}, f32[16,384]{1,0:T(8,128)}, u32[]{:S(2)}) copy-start(f32[16,384]{1,0:T(8,128)} %param.11) | copy-start | bytes 73732
  48.2 1.7 %copy-start.1 = (f32[16,96,384]{2,1,0:T(8,128)S(1)}, f32[16,96,384]{2,1,0:T(8,128)}, u32[]{:S(2)}) copy-start(f32[16,96,384]{2,1,0:T(8,128)} %param.10) | copy-start | bytes 7077892
  89.5 2.3 %copy-start.7 = (f32[4,48]{1,0:T(4,128)}, f32[4,48]{1,0:T(4,128)S(1)}, u32[]{:S(2)}) copy-start(f32[4,48]{1,0:T(4,128)S(1)} %multiply_add_fusion.2) | copy-start | bytes 2308
where the time goes:
time: 92.1 us; the launch traced here: 91.8 us
  blocking collectives  78.3 us (85%)
  matrix products  11.7 us (13%)
    psum x2, blocking collectives, local(): floor_load = lax.psum(partial_load, 'zone')  30.8 us
    all_gather x2, blocking collectives, local(): floor_bound = lax.all_gather(bound, 'zone', axis=0, tiled=True)  29.7 us
    psum x2, blocking collectives, local(): total = lax.psum(floor_load, 'floor')  17.8 us
    dot_general x2, matrix products, local(): jnp.einsum('zkv,zv->zk', plant_map, control, precision=lax.Precision.HIGH...  7 us
    dot_general x2, matrix products, local(): jnp.einsum('zkv,zk->zv', factor, target, precision=lax.Precision.HIGHEST)  2.88 us

commit v1 on v0

--- a/solution.py
+++ b/solution.py
@@ -39,7 +39,8 @@
         shares = outputs[:, :HORIZON]
         bound = outputs[:, HORIZON:]
         partial_load = jnp.dot(onehot.T, shares, precision=lax.Precision.HIGHEST)
-        floor_load = lax.psum(partial_load, "zone")
+        pieces = lax.all_gather(partial_load, "zone")
+        floor_load = jnp.sum(pieces, axis=0)
         total = lax.psum(floor_load, "floor")
         excess = (total - demand) * (LOOPS / zones_all)
         shift = jnp.dot(onehot, excess + price, precision=lax.Precision.HIGHEST)

time: 92.1 us -> 86.8 us (0.942)
  blocking collectives: 78.3 us -> 73.1 us
    psum x2 -> x0, blocking collectives: 30.8 us -> none  [local(): floor_load = lax.psum(partial_load, 'zone')]
    all_gather x0 -> x2, blocking collectives: none -> 25.5 us  [local(): pieces = lax.all_gather(partial_load, 'zone')]
where the time goes in v1:
time: 86.8 us; the launch traced here: 86.6 us
  blocking collectives  73.1 us (84%)
  matrix products  11.7 us (13%)
  other arithmetic  0.91 us (1%)
    all_gather x2, blocking collectives, local(): floor_bound = lax.all_gather(bound, 'zone', axis=0, tiled=True)  29.7 us
    all_gather x2, blocking collectives, local(): pieces = lax.all_gather(partial_load, 'zone')  25.5 us
    psum x2, blocking collectives, local(): total = lax.psum(floor_load, 'floor')  17.9 us
    dot_general x2, matrix products, local(): jnp.einsum('zkv,zv->zk', plant_map, control, precision=lax.Precision.HIGH...  7 us
    dot_general x2, matrix products, local(): jnp.einsum('zkv,zk->zv', factor, target, precision=lax.Precision.HIGHEST)  2.88 us

profile of v1, /device:TPU:0, one launch (start us, length us, event | category | flops | bytes accessed | tf_op | source)
XLA Modules:
  0.0 86.6 jit_solution(2132968364415672605)
XLA Ops:
  0.6 0.0 copy-start
  0.6 0.0 copy-start.3
  0.7 0.0 copy-start.4
  0.7 0.0 copy-start.8
  0.7 0.0 copy-start.5
  0.7 0.0 copy-start.6
  0.7 0.0 copy-start.2
  0.7 4.4 %fusion.5 = f32[16,1,96]{2,1,0:T(1,128)S(1)} fusion(f32[16,96,384]{2,1,0:T(8,128)} %param.10, f32[16,384,1]{1,0,2:T(8,128)} %bitcast.47), kind=kOutput, calls=%fused_computation.13 | convolution fusion | flops 7077888 | bytes 2390016 | tf_op jit(solution)/shard_map/zkv,zv->zk/dot_general | solution.py:38
  5.1 0.1 slice.17
  5.2 15.7 %all_gather.20 = f32[128,48]{1,0:T(8,128)S(1)} all-gather(f32[16,48]{1,0:T(8,128)S(1)} %slice.17), channel_id=1, replica_groups=mesh['floor'=4,'zone'=8] {'zone'}, dimensions={0}, use_global_device_ids=true | all-gather | bytes 27648 | tf_op jit(solution)/shard_map/all_gather | solution.py:49
  20.9 0.0 copy-done.4
  20.9 0.1 convert_reduce_fusion
  21.0 0.0 copy-done.3
  21.0 0.2 multiply_subtract_fusion.1
  21.1 0.0 copy-done.8
  21.1 0.3 convolution_bitcast_fusion.1
  21.4 12.8 %all-gather.2 = f32[8,4,48]{2,1,0:T(4,128)S(1)} all-gather(f32[1,4,48]{2,1,0:T(4,128)S(1)} %convolution_bitcast_fusion.1), channel_id=2, replica_groups=mesh['floor'=4,'zone'=8] {'zone'}, dimensions={0}, use_global_device_ids=true | all-gather | bytes 6912 | tf_op jit(solution)/shard_map/all_gather | solution.py:42
  34.2 9.9 %psum.14 = f32[4,48]{1,0:T(4,128)S(1)} all-reduce(f32[4,48]{1,0:T(4,128)S(1)} %reduce_sum.27), channel_id=1, replica_groups=mesh['floor'=4,'zone'=8] {'floor'}, use_global_device_ids=true, to_apply=%region_1.0 | all-reduce | flops 192 | bytes 1536 | tf_op jit(solution)/shard_map/psum | solution.py:44
  44.1 0.0 copy-done.5
  44.1 0.0 copy-done.6
  44.1 0.0 copy-start.1
  44.1 0.2 convolution_subtract_fusion.1
  44.3 0.1 pad_maximum_fusion
  44.4 0.0 copy-done
  44.4 1.4 %fusion.22 = f32[16,1,384]{2,1,0:T(1,128)S(1)} fusion(f32[16,96,1]{1,2,0:T(1,128)S(1)} %bitcast.45, f32[16,96,384]{2,1,0:T(8,128)S(1)} %copy-done), kind=kOutput, calls=%fused_computation.39 | convolution fusion | flops 7077888 | bytes 2390016 | tf_op jit(solution)/shard_map/zkv,zk->zv/dot_general | solution.py:56
  45.8 0.0 copy-done.2
  45.8 0.0 copy-done.1
  45.9 2.6 %fusion.3 = f32[16,1,96]{2,1,0:T(1,128)S(1)} fusion(f32[16,96,384]{2,1,0:T(8,128)S(1)} %copy-done.1, f32[16,384,1]{1,0,2:T(8,128)S(1)} %fusion.2), kind=kOutput, calls=%fused_computation.11 | convolution fusion | flops 7077888 | bytes 2390016 | tf_op jit(solution)/shard_map/zkv,zv->zk/dot_general | solution.py:38
  48.4 0.1 slice.19
  48.5 14.0 %all_gather.23 = f32[128,48]{1,0:T(8,128)S(1)} all-gather(f32[16,48]{1,0:T(8,128)S(1)} %slice.19), channel_id=1, replica_groups=mesh['floor'=4,'zone'=8] {'zone'}, dimensions={0}, use_global_device_ids=true | all-gather | bytes 27648 | tf_op jit(solution)/shard_map/all_gather | solution.py:49
  62.5 0.8 multiply_add_fusion
  63.3 0.3 convolution_bitcast_fusion
  63.5 12.8 %all-gather.3 = f32[8,4,48]{2,1,0:T(4,128)S(1)} all-gather(f32[1,4,48]{2,1,0:T(4,128)S(1)} %convolution_bitcast_fusion), channel_id=3, replica_groups=mesh['floor'=4,'zone'=8] {'zone'}, dimensions={0}, use_global_device_ids=true | all-gather | bytes 6912 | tf_op jit(solution)/shard_map/all_gather | solution.py:42
  76.3 8.0 %psum.15 = f32[4,48]{1,0:T(4,128)S(1)} all-reduce(f32[4,48]{1,0:T(4,128)S(1)} %reduce_sum.33), channel_id=1, replica_groups=mesh['floor'=4,'zone'=8] {'floor'}, use_global_device_ids=true, to_apply=%region_4.0 | all-reduce | flops 192 | bytes 1536 | tf_op jit(solution)/shard_map/psum | solution.py:44
  84.3 0.0 copy-start.7
  84.3 0.2 convolution_subtract_fusion
  84.5 0.1 pad_maximum_fusion.1
  84.6 1.4 %fusion.23 = f32[16,1,384]{2,1,0:T(1,128)S(1)} fusion(f32[16,96,1]{1,2,0:T(1,128)S(1)} %bitcast.46, f32[16,96,384]{2,1,0:T(8,128)S(1)} %copy-done), kind=kOutput, calls=%fused_computation.40 | convolution fusion | flops 7077888 | bytes 2390016 | tf_op jit(solution)/shard_map/zkv,zk->zv/dot_general | solution.py:56
  86.0 0.6 fusion
  86.6 0.0 copy-done.7
  (4 shorter events, 0.1 us)
Async XLA Ops:
  0.6 43.7 %copy-start = (f32[16,96,384]{2,1,0:T(8,128)S(1)}, f32[16,96,384]{2,1,0:T(8,128)}, u32[]{:S(2)}) copy-start(f32[16,96,384]{2,1,0:T(8,128)} %param.9) | copy-start | bytes 7077892
  0.6 20.3 %copy-start.3 = (f32[16,48]{1,0:T(8,128)S(1)}, f32[16,48]{1,0:T(8,128)}, u32[]{:S(2)}) copy-start(f32[16,48]{1,0:T(8,128)} %param.15) | copy-start | bytes 9220
  0.7 20.2 %copy-start.4 = (s32[16,4]{0,1:T(4,128)S(1)}, s32[16,4]{0,1:T(4,128)}, u32[]{:S(2)}) copy-start(s32[16,4]{0,1:T(4,128)} %param.16) | copy-start | bytes 772
  0.7 20.5 %copy-start.8 = (s32[16]{0:T(128)S(1)}, s32[16]{0:T(128)}, u32[]{:S(2)}) copy-start(s32[16]{0:T(128)} %param.17) | copy-start | bytes 196
  0.7 43.4 %copy-start.5 = (f32[4,48]{1,0:T(4,128)S(1)}, f32[4,48]{1,0:T(4,128)}, u32[]{:S(2)}) copy-start(f32[4,48]{1,0:T(4,128)} %param.14) | copy-start | bytes 2308
  0.7 43.4 %copy-start.6 = (f32[4,48]{1,0:T(4,128)S(1)}, f32[4,48]{1,0:T(4,128)}, u32[]{:S(2)}) copy-start(f32[4,48]{1,0:T(4,128)} %param.13) | copy-start | bytes 2308
  0.7 45.1 %copy-start.2 = (f32[16,384]{1,0:T(8,128)S(1)}, f32[16,384]{1,0:T(8,128)}, u32[]{:S(2)}) copy-start(f32[16,384]{1,0:T(8,128)} %param.11) | copy-start | bytes 73732
  44.1 1.7 %copy-start.1 = (f32[16,96,384]{2,1,0:T(8,128)S(1)}, f32[16,96,384]{2,1,0:T(8,128)}, u32[]{:S(2)}) copy-start(f32[16,96,384]{2,1,0:T(8,128)} %param.10) | copy-start | bytes 7077892
  84.3 2.3 %copy-start.7 = (f32[4,48]{1,0:T(4,128)}, f32[4,48]{1,0:T(4,128)S(1)}, u32[]{:S(2)}) copy-start(f32[4,48]{1,0:T(4,128)S(1)} %multiply_add_fusion.2) | copy-start | bytes 2308
